TPU v7x, 256 devices: a whole 4x4x8 slice. The times are simulated.
256 devices in a mesh: gx: 8 (over y, x_lo), gy: 16 (over z, core), gz: 2 (over x_hi).
Axes of the slice: x: 4 (x_hi: 2, x_lo: 2; x = x_hi * 2 + x_lo), y: 4, z: 8, core: 2. Of those that a mesh axis runs over, the one named last changes fastest.
Arguments:
- starting_kelvin: float32 [16, 128, 4096], P(None, 'gx', ('gy', 'gz')), may hold values from -6 to 6
- substance_label: int32 [16, 128, 4096], P(None, 'gx', ('gy', 'gz')), may hold values from 0 to 3
- voxel_source_patch: int32 [16, 128, 4096], P(None, 'gx', ('gy', 'gz')), may hold values from 0 to 15
- substance_traits: float32 [4, 4], replicated, may hold values from 0.5 to 2
- patch_source_intensity: float32 [16], replicated, may hold values from 0 to 8
Outputs:
- warmed_result: float32 [16, 128, 4096], P(None, 'gx', ('gy', 'gz'))
- solution: float32 [3, 16, 128, 4096], P(None, 'gz', 'gx', 'gy')
- residual: float32 [3, 16, 128, 4096], P(None, 'gz', 'gx', 'gy')
All inputs are finite; a program needn't handle non-finite values.
Results may differ from a plain program's by a relative error of at most 0.0029.
Values sent between devices are 32-bit elements; how exact they have to be, the bound alone decides.
A program may use at most 64 MiB of HBM per device.

v0:
```python
import jax
import jax.numpy as jnp
from jax import lax
from jax.sharding import Mesh
from jax.sharding import PartitionSpec as P

HEAT_STEPS = 2
ITERS = 3
GX_GY_GZ = ("gx_0", "gx_1", "gy_0", "gy_1", "gz")
GX = ("gx_0", "gx_1")
GY_GZ = ("gy_0", "gy_1", "gz")
GY = ("gy_0", "gy_1")
time_step = 0.03
anchor_scale = 0.5
strain_gain = 2.0


def over_axes(value, axes):
    for axis in axes:
        value = lax.psum(value, axis)
    return value


def padded(value, sides, width):
    for axis, dim in sides:
        devices, length = (lax.axis_size(axis), value.shape[dim])
        up = [(i, (i + 1) % devices) for i in range(devices - 1)]
        down = [(j, i) for i, j in up]
        last = lax.slice_in_dim(value, length - width, length, axis=dim)
        initial = lax.slice_in_dim(value, 0, width, axis=dim)
        before = lax.ppermute(last, axis, up)
        after = lax.ppermute(initial, axis, down)
        value = jnp.concatenate([before, value, after], axis=dim)
    return value


def lookup(identity, table, count):
    summed = jnp.zeros(identity.shape, jnp.float32)
    for number in range(count):
        summed = summed + jnp.where(identity == number, table[number], jnp.float32(0.0))
    return summed


def conduct(own, other):
    return 2.0 * own * other / jnp.maximum(own + other, 0.25)


def heat_step(padded_temp, padded_cond, power, inverse_cap):
    centre = padded_temp[:, 1:-1, 1:-1]
    own = padded_cond[:, 1:-1, 1:-1]
    layers, rows, columns = centre.shape
    heat_flux = jnp.zeros_like(centre)
    for row_offset, column_offset in ((0, 1), (2, 1), (1, 0), (1, 2)):
        neighbour = padded_temp[
            :, row_offset : row_offset + rows, column_offset : column_offset + columns
        ]
        other = padded_cond[
            :, row_offset : row_offset + rows, column_offset : column_offset + columns
        ]
        heat_flux = heat_flux + conduct(own, other) * (neighbour - centre)
    vertical_temp = jnp.pad(centre, ((1, 1), (0, 0), (0, 0)))
    vertical_cond = jnp.pad(own, ((1, 1), (0, 0), (0, 0)))
    for layer_offset in (0, 2):
        other = vertical_cond[layer_offset : layer_offset + layers]
        neighbour = vertical_temp[layer_offset : layer_offset + layers]
        heat_flux = heat_flux + conduct(own, other) * (neighbour - centre)
    return centre + time_step * inverse_cap * (heat_flux + power)


def crop(array, margin):
    return array[:, margin : array.shape[1] - margin, margin : array.shape[2] - margin]


def neighbour_offsets():
    listed = []
    for along_z in (-1, 0, 1):
        for along_x in (-1, 0, 1):
            for along_y in (-1, 0, 1):
                if along_z != 0 or along_x != 0 or along_y != 0:
                    listed.append((along_z, along_x, along_y))
    return listed


def apply_operator(field, padded_field, modulus, padded_modulus):
    layers, rows, columns = modulus.shape
    parts = [
        anchor_scale * modulus * field[0],
        anchor_scale * modulus * field[1],
        anchor_scale * modulus * field[2],
    ]
    for along_z, along_x, along_y in neighbour_offsets():
        length_sq = along_z * along_z + along_x * along_x + along_y * along_y
        window = (
            slice(1 + along_z, 1 + along_z + layers),
            slice(1 + along_x, 1 + along_x + rows),
            slice(1 + along_y, 1 + along_y + columns),
        )
        weight = 0.5 / length_sq * (modulus + padded_modulus[window])
        change = [field[index_c] - padded_field[index_c][window] for index_c in range(3)]
        projected = (along_z * change[0] + along_x * change[1] + along_y * change[2]) / length_sq
        for index_c, direction_part in enumerate((along_z, along_x, along_y)):
            parts[index_c] = parts[index_c] + weight * (
                0.5 * change[index_c] + direction_part * projected
            )
    return jnp.stack(parts)


def thermal_load(modulus, padded_modulus, strain, padded_strain):
    layers, rows, columns = modulus.shape
    parts = [jnp.zeros_like(modulus), jnp.zeros_like(modulus), jnp.zeros_like(modulus)]
    for along_z, along_x, along_y in neighbour_offsets():
        length_sq = along_z * along_z + along_x * along_x + along_y * along_y
        window = (
            slice(1 + along_z, 1 + along_z + layers),
            slice(1 + along_x, 1 + along_x + rows),
            slice(1 + along_y, 1 + along_y + columns),
        )
        weight = 0.5 / length_sq * (modulus + padded_modulus[window])
        pushing = weight * (0.5 * (strain + padded_strain[window]))
        for index_c, direction_part in enumerate((along_z, along_x, along_y)):
            if direction_part != 0:
                parts[index_c] = parts[index_c] - strain_gain * direction_part * pushing
    return jnp.stack(parts)


def two_products(residual, image):
    return (
        over_axes(jnp.sum(residual * residual), GX_GY_GZ),
        over_axes(jnp.sum(residual * image), GX_GY_GZ),
    )


def per_device(
    starting_kelvin, substance_label, voxel_source_patch, substance_traits, patch_source_intensity
):
    count = substance_traits.shape[1]
    diffusive_coefficient = lookup(substance_label, substance_traits[0], count)
    inverse_cap = 1.0 / lookup(substance_label, substance_traits[1], count)
    power = lookup(voxel_source_patch, patch_source_intensity, patch_source_intensity.shape[0])
    padded_array = padded(
        jnp.stack([starting_kelvin, diffusive_coefficient, power, inverse_cap]),
        ((GX, 2), (GY_GZ, 3)),
        HEAT_STEPS,
    )
    warmed_result = padded_array[0]
    for number in range(HEAT_STEPS):
        warmed_result = heat_step(
            warmed_result,
            crop(padded_array[1], number),
            crop(padded_array[2], number + 1),
            crop(padded_array[3], number + 1),
        )
    modulus = lookup(substance_label, substance_traits[2], count)
    strain = lookup(substance_label, substance_traits[3], count) * warmed_result
    fields = jnp.stack([modulus, strain])
    fields = lax.all_to_all(fields, "gz", split_axis=1, concat_axis=3, tiled=True)
    padded_fields = padded(fields, ((GX, 2), (GY, 3), ("gz", 1)), 1)

    def extend(field):
        return padded(field, ((GX, 2), (GY, 3), ("gz", 1)), 1)

    modulus = fields[0]
    padded_modulus = padded_fields[0]
    load = thermal_load(modulus, padded_modulus, fields[1], padded_fields[1])

    def operate(field):
        return apply_operator(field, extend(field), modulus, padded_modulus)

    solution = jnp.zeros_like(load)
    residual = load
    image = operate(residual)
    norm_now, product = two_products(residual, image)
    alpha = norm_now / product
    direction, along_image = (residual, image)
    for number in range(ITERS):
        solution = solution + alpha * direction
        residual = residual - alpha * along_image
        if number + 1 < ITERS:
            image = operate(residual)
            norm_next, product = two_products(residual, image)
            ratio = norm_next / norm_now
            alpha = norm_next / (product - ratio * norm_next / alpha)
            direction = residual + ratio * direction
            along_image = image + ratio * along_image
            norm_now = norm_next
    return (warmed_result, solution, residual)


def solution(mesh):
    split = Mesh(
        mesh.devices.reshape(4, 2, 8, 2, mesh.shape["gz"]), ("gx_0", "gx_1", "gy_0", "gy_1", "gz")
    )
    placed = (P(None, GX, GY_GZ), P(None, GX, GY_GZ), P(None, GX, GY_GZ), P(), P())
    return jax.shard_map(
        per_device,
        mesh=split,
        in_specs=placed,
        out_specs=(P(None, GX, GY_GZ), P(None, "gz", GX, GY), P(None, "gz", GX, GY)),
        check_vma=False,
    )
```

profile of v0, /device:TPU:1, one launch (start us, length us, event | category | flops | bytes accessed | tf_op | source)
XLA Modules:
  0.0 349.6 jit_solution(3957960679545552829)
XLA Ops:
  8.0 5.2 %add_bitcast_fusion.11 = (f32[1,16,16,128]{3,1,2,0:T(8,128)S(1)}, f32[1,16,16,128]{3,1,2,0:T(8,128)S(1)}) fusion(pred[16,16,128]{2,0,1:T(8,128)(4,1)S(1)} %get-tuple-element.98, pred[16,16,128]{2,0,1:T(8,128)(4,1)S(1)} %get-tuple-element.97, pred[16,16,128]{2,0,1:T(8,128)(4,1)S(1)} %get-tuple-element.96, pred[16,16,128]{2,0,1:T(8,128)(4,1)S(1)} %get-tuple-element.95, ...), kind=kLoop, calls=%fused_computation.621 | loop fusion | flops 491520 | bytes 393248 | tf_op jit(solution)/shard_map/stack | solution.py:141
  13.2 11.3 %copy_bitcast_fusion = (f32[1,16,16,128]{3,1,2,0:T(8,128)S(1)}, f32[1,16,16,128]{3,1,2,0:T(8,128)S(1)}) fusion(f32[16,16,128]{2,1,0:T(8,128)} %param.5, f32[]{:T(128)} %bitcast.21, f32[]{:T(128)} %bitcast.20, f32[]{:T(128)} %bitcast.19, f32[]{:T(128)} %bitcast.18, f32[]{:T(128)} %bitcast.17, f32[]{:T(128)} %bitcast.16, f32[]{:T(128)} %bitcast.15, ...), kind=kLoop, calls=%fused_computation.521 | loop fusion | flops 1540096 | bytes 524352 | tf_op jit(solution)/shard_map/stack | solution.py:141
  34.2 4.5 %collective-permute-start.2 = (f32[4,16,20,2]{2,1,3,0:T(8,128)S(1)}, f32[4,16,20,2]{2,1,3,0:T(8,128)S(1)}, u32[]{:S(2)}, u32[]{:S(2)}) collective-permute-start(f32[4,16,20,2]{2,1,3,0:T(8,128)S(1)} %copy.202), channel_id=1, source_target_pairs={{0,1},{1,2},{2,3},{3,4},{4,5},{5,6},{6,7},{7,8},{8,9},{9,10},{10,1... | collective-permute-start | bytes 30728 | tf_op jit(solution)/shard_map/ppermute | solution.py:31
  52.1 12.7 %all_to_all.18 = f32[2,16,16,128]{3,2,0,1:T(8,128)S(1)} all-to-all(f32[2,16,16,128]{3,2,0,1:T(8,128)S(1)} %copy.206), channel_id=1, replica_groups=mesh['gx_0'=4,'gx_1'=2,'gy_0'=8,'gy_1'=2,'gz'=2] {'gz'}, dimensions={1} | all-to-all | bytes 524288 | tf_op jit(solution)/shard_map/all_to_all | solution.py:156
  73.4 5.2 %collective-permute-start.6 = (f32[2,8,18,1]{3,2,1,0:T(8,128)S(1)}, f32[2,8,18,1]{3,2,1,0:T(8,128)S(1)}, u32[]{:S(2)}, u32[]{:S(2)}) collective-permute-start(f32[2,8,18,1]{3,2,1,0:T(8,128)S(1)} %get-tuple-element.142), channel_id=1, source_target_pairs={{0,2},{2,4},{4,6},{6,8},{8,10},{10,12},{12,14},{14,16},{16,18},{18... | collective-permute-start | bytes 3464 | tf_op jit(solution)/shard_map/ppermute | solution.py:31
  81.2 4.4 %collective-permute-done.7 = f32[2,8,18,1]{3,2,1,0:T(8,128)S(1)} collective-permute-done((f32[2,8,18,1]{3,2,1,0:T(8,128)S(1)}, f32[2,8,18,1]{3,2,1,0:T(8,128)S(1)}, u32[]{:S(2)}, u32[]{:S(2)}) %collective-permute-start.7) | collective-permute-done | bytes 1184 | tf_op jit(solution)/shard_map/ppermute | solution.py:32
  89.5 4.8 %collective-permute-done.9 = f32[2,1,18,258]{3,2,1,0:T(8,128)S(1)} collective-permute-done((f32[2,1,18,258]{3,2,1,0:T(8,128)S(1)}, f32[2,1,18,258]{3,2,1,0:T(8,128)S(1)}, u32[]{:S(2)}, u32[]{:S(2)}) %collective-permute-start.9) | collective-permute-done | bytes 37184 | tf_op jit(solution)/shard_map/ppermute | solution.py:32
  105.3 4.4 %collective-permute-start.12 = (f32[3,8,18,1]{3,2,1,0:T(8,128)S(1)}, f32[3,8,18,1]{3,2,1,0:T(8,128)S(1)}, u32[]{:S(2)}, u32[]{:S(2)}) collective-permute-start(f32[3,8,18,1]{3,2,1,0:T(8,128)S(1)} %get-tuple-element.130), channel_id=1, source_target_pairs={{0,2},{2,4},{4,6},{6,8},{8,10},{10,12},{12,14},{14,16},{16,18},{18... | collective-permute-start | bytes 5192 | tf_op jit(solution)/shard_map/ppermute | solution.py:31
  113.3 4.4 %collective-permute-done.13 = f32[3,8,18,1]{3,2,1,0:T(8,128)S(1)} collective-permute-done((f32[3,8,18,1]{3,2,1,0:T(8,128)S(1)}, f32[3,8,18,1]{3,2,1,0:T(8,128)S(1)}, u32[]{:S(2)}, u32[]{:S(2)}) %collective-permute-start.13) | collective-permute-done | bytes 1760 | tf_op jit(solution)/shard_map/ppermute | solution.py:32
  121.6 5.3 %collective-permute-done.15 = f32[3,1,18,258]{3,2,1,0:T(8,128)S(1)} collective-permute-done((f32[3,1,18,258]{3,2,1,0:T(8,128)S(1)}, f32[3,1,18,258]{3,2,1,0:T(8,128)S(1)}, u32[]{:S(2)}, u32[]{:S(2)}) %collective-permute-start.15) | collective-permute-done | bytes 55760 | tf_op jit(solution)/shard_map/ppermute | solution.py:32
  136.0 7.9 %all-reduce.9 = (f32[]{:T(128)}, f32[]{:T(128)}) all-reduce(f32[]{:T(128)} %get-tuple-element.17, f32[]{:T(128)} %get-tuple-element.16), channel_id=1, replica_groups=mesh['gx_0'=4,'gx_1'=2,'gy_0'=8,'gy_1'=2,'gz'=2] {'gx_0'}, use_global_device_ids=true, to_apply=%region_1.2 | all-reduce | flops 2 | bytes 16 | tf_op jit(solution)/shard_map/psum | solution.py:20
  143.9 4.4 %all-reduce.18 = (f32[]{:T(128)}, f32[]{:T(128)}) all-reduce(f32[]{:T(128)} %get-tuple-element.28, f32[]{:T(128)} %get-tuple-element.29), channel_id=1, replica_groups=mesh['gx_0'=4,'gx_1'=2,'gy_0'=8,'gy_1'=2,'gz'=2] {'gx_1'}, use_global_device_ids=true, to_apply=%region_2.3 | all-reduce | flops 2 | bytes 16 | tf_op jit(solution)/shard_map/psum | solution.py:20
  148.2 17.7 %all-reduce.6 = (f32[]{:T(128)}, f32[]{:T(128)}) all-reduce(f32[]{:T(128)} %get-tuple-element.46, f32[]{:T(128)} %get-tuple-element.47), channel_id=1, replica_groups=mesh['gx_0'=4,'gx_1'=2,'gy_0'=8,'gy_1'=2,'gz'=2] {'gy_0'}, use_global_device_ids=true, to_apply=%region_3.4 | all-reduce | flops 2 | bytes 16 | tf_op jit(solution)/shard_map/psum | solution.py:20
  166.0 8.6 %all-reduce.15 = (f32[]{:T(128)}, f32[]{:T(128)}) all-reduce(f32[]{:T(128)} %get-tuple-element.22, f32[]{:T(128)} %get-tuple-element.23), channel_id=1, replica_groups=mesh['gx_0'=4,'gx_1'=2,'gy_0'=8,'gy_1'=2,'gz'=2] {'gy_1'}, use_global_device_ids=true, to_apply=%region_4.5 | all-reduce | flops 2 | bytes 16 | tf_op jit(solution)/shard_map/psum | solution.py:20
  174.5 5.9 %all-reduce.12 = (f32[]{:T(128)}, f32[]{:T(128)}) all-reduce(f32[]{:T(128)} %get-tuple-element.40, f32[]{:T(128)} %get-tuple-element.41), channel_id=1, replica_groups=mesh['gx_0'=4,'gx_1'=2,'gy_0'=8,'gy_1'=2,'gz'=2] {'gz'}, use_global_device_ids=true, to_apply=%region_5.6 | all-reduce | flops 2 | bytes 16 | tf_op jit(solution)/shard_map/psum | solution.py:20
  190.4 5.2 %collective-permute-start.18 = (f32[3,8,18,1]{3,2,1,0:T(8,128)S(1)}, f32[3,8,18,1]{3,2,1,0:T(8,128)S(1)}, u32[]{:S(2)}, u32[]{:S(2)}) collective-permute-start(f32[3,8,18,1]{3,2,1,0:T(8,128)S(1)} %get-tuple-element.128), channel_id=1, source_target_pairs={{0,2},{2,4},{4,6},{6,8},{8,10},{10,12},{12,14},{14,16},{16,18},{18... | collective-permute-start | bytes 5192 | tf_op jit(solution)/shard_map/ppermute | solution.py:31
  199.2 4.4 %collective-permute-done.19 = f32[3,8,18,1]{3,2,1,0:T(8,128)S(1)} collective-permute-done((f32[3,8,18,1]{3,2,1,0:T(8,128)S(1)}, f32[3,8,18,1]{3,2,1,0:T(8,128)S(1)}, u32[]{:S(2)}, u32[]{:S(2)}) %collective-permute-start.19) | collective-permute-done | bytes 1760 | tf_op jit(solution)/shard_map/ppermute | solution.py:32
  207.7 5.3 %collective-permute-done.21 = f32[3,1,18,258]{3,2,1,0:T(8,128)S(1)} collective-permute-done((f32[3,1,18,258]{3,2,1,0:T(8,128)S(1)}, f32[3,1,18,258]{3,2,1,0:T(8,128)S(1)}, u32[]{:S(2)}, u32[]{:S(2)}) %collective-permute-start.21) | collective-permute-done | bytes 55760 | tf_op jit(solution)/shard_map/ppermute | solution.py:32
  220.2 7.1 %all-reduce.8 = (f32[]{:T(128)}, f32[]{:T(128)}) all-reduce(f32[]{:T(128)} %get-tuple-element.15, f32[]{:T(128)} %get-tuple-element.14), channel_id=1, replica_groups=mesh['gx_0'=4,'gx_1'=2,'gy_0'=8,'gy_1'=2,'gz'=2] {'gx_0'}, use_global_device_ids=true, to_apply=%region_13.14 | all-reduce | flops 2 | bytes 16 | tf_op jit(solution)/shard_map/psum | solution.py:20
  227.3 4.4 %all-reduce.17 = (f32[]{:T(128)}, f32[]{:T(128)}) all-reduce(f32[]{:T(128)} %get-tuple-element.26, f32[]{:T(128)} %get-tuple-element.27), channel_id=1, replica_groups=mesh['gx_0'=4,'gx_1'=2,'gy_0'=8,'gy_1'=2,'gz'=2] {'gx_1'}, use_global_device_ids=true, to_apply=%region_14.15 | all-reduce | flops 2 | bytes 16 | tf_op jit(solution)/shard_map/psum | solution.py:20
  231.7 14.0 %all-reduce.5 = (f32[]{:T(128)}, f32[]{:T(128)}) all-reduce(f32[]{:T(128)} %get-tuple-element.44, f32[]{:T(128)} %get-tuple-element.45), channel_id=1, replica_groups=mesh['gx_0'=4,'gx_1'=2,'gy_0'=8,'gy_1'=2,'gz'=2] {'gy_0'}, use_global_device_ids=true, to_apply=%region_15.16 | all-reduce | flops 2 | bytes 16 | tf_op jit(solution)/shard_map/psum | solution.py:20
  245.7 9.5 %all-reduce.14 = (f32[]{:T(128)}, f32[]{:T(128)}) all-reduce(f32[]{:T(128)} %get-tuple-element.20, f32[]{:T(128)} %get-tuple-element.21), channel_id=1, replica_groups=mesh['gx_0'=4,'gx_1'=2,'gy_0'=8,'gy_1'=2,'gz'=2] {'gy_1'}, use_global_device_ids=true, to_apply=%region_16.17 | all-reduce | flops 2 | bytes 16 | tf_op jit(solution)/shard_map/psum | solution.py:20
  255.2 6.1 %all-reduce.11 = (f32[]{:T(128)}, f32[]{:T(128)}) all-reduce(f32[]{:T(128)} %get-tuple-element.38, f32[]{:T(128)} %get-tuple-element.39), channel_id=1, replica_groups=mesh['gx_0'=4,'gx_1'=2,'gy_0'=8,'gy_1'=2,'gz'=2] {'gz'}, use_global_device_ids=true, to_apply=%region_17.18 | all-reduce | flops 2 | bytes 16 | tf_op jit(solution)/shard_map/psum | solution.py:20
  269.4 4.2 %collective-permute-done.23 = f32[3,8,1,256]{3,2,1,0:T(1,128)S(1)} collective-permute-done((f32[3,8,1,256]{3,2,1,0:T(1,128)S(1)}, f32[3,8,1,256]{3,2,1,0:T(1,128)S(1)}, u32[]{:S(2)}, u32[]{:S(2)}) %collective-permute-start.23) | collective-permute-done | bytes 24608 | tf_op jit(solution)/shard_map/ppermute | solution.py:32
  273.8 5.0 %collective-permute-start.24 = (f32[3,8,18,1]{3,2,1,0:T(8,128)S(1)}, f32[3,8,18,1]{3,2,1,0:T(8,128)S(1)}, u32[]{:S(2)}, u32[]{:S(2)}) collective-permute-start(f32[3,8,18,1]{3,2,1,0:T(8,128)S(1)} %get-tuple-element.126), channel_id=1, source_target_pairs={{0,2},{2,4},{4,6},{6,8},{8,10},{10,12},{12,14},{14,16},{16,18},{18... | collective-permute-start | bytes 5192 | tf_op jit(solution)/shard_map/ppermute | solution.py:31
  282.4 4.4 %collective-permute-done.25 = f32[3,8,18,1]{3,2,1,0:T(8,128)S(1)} collective-permute-done((f32[3,8,18,1]{3,2,1,0:T(8,128)S(1)}, f32[3,8,18,1]{3,2,1,0:T(8,128)S(1)}, u32[]{:S(2)}, u32[]{:S(2)}) %collective-permute-start.25) | collective-permute-done | bytes 1760 | tf_op jit(solution)/shard_map/ppermute | solution.py:32
  290.8 5.0 %collective-permute-done.27 = f32[3,1,18,258]{3,2,1,0:T(8,128)S(1)} collective-permute-done((f32[3,1,18,258]{3,2,1,0:T(8,128)S(1)}, f32[3,1,18,258]{3,2,1,0:T(8,128)S(1)}, u32[]{:S(2)}, u32[]{:S(2)}) %collective-permute-start.27) | collective-permute-done | bytes 55760 | tf_op jit(solution)/shard_map/ppermute | solution.py:32
  303.1 7.6 %all-reduce.7 = (f32[]{:T(128)}, f32[]{:T(128)}) all-reduce(f32[]{:T(128)} %get-tuple-element.13, f32[]{:T(128)} %get-tuple-element.12), channel_id=1, replica_groups=mesh['gx_0'=4,'gx_1'=2,'gy_0'=8,'gy_1'=2,'gz'=2] {'gx_0'}, use_global_device_ids=true, to_apply=%region_25.26 | all-reduce | flops 2 | bytes 16 | tf_op jit(solution)/shard_map/psum | solution.py:20
  310.7 4.4 %all-reduce.16 = (f32[]{:T(128)}, f32[]{:T(128)}) all-reduce(f32[]{:T(128)} %get-tuple-element.24, f32[]{:T(128)} %get-tuple-element.25), channel_id=1, replica_groups=mesh['gx_0'=4,'gx_1'=2,'gy_0'=8,'gy_1'=2,'gz'=2] {'gx_1'}, use_global_device_ids=true, to_apply=%region_26.27 | all-reduce | flops 2 | bytes 16 | tf_op jit(solution)/shard_map/psum | solution.py:20
  315.1 14.0 %all-reduce.4 = (f32[]{:T(128)}, f32[]{:T(128)}) all-reduce(f32[]{:T(128)} %get-tuple-element.42, f32[]{:T(128)} %get-tuple-element.43), channel_id=1, replica_groups=mesh['gx_0'=4,'gx_1'=2,'gy_0'=8,'gy_1'=2,'gz'=2] {'gy_0'}, use_global_device_ids=true, to_apply=%region_27.28 | all-reduce | flops 2 | bytes 16 | tf_op jit(solution)/shard_map/psum | solution.py:20
  329.1 9.5 %all-reduce.13 = (f32[]{:T(128)}, f32[]{:T(128)}) all-reduce(f32[]{:T(128)} %get-tuple-element.18, f32[]{:T(128)} %get-tuple-element.19), channel_id=1, replica_groups=mesh['gx_0'=4,'gx_1'=2,'gy_0'=8,'gy_1'=2,'gz'=2] {'gy_1'}, use_global_device_ids=true, to_apply=%region_28.29 | all-reduce | flops 2 | bytes 16 | tf_op jit(solution)/shard_map/psum | solution.py:20
  338.7 5.9 %all-reduce.10 = (f32[]{:T(128)}, f32[]{:T(128)}) all-reduce(f32[]{:T(128)} %get-tuple-element.36, f32[]{:T(128)} %get-tuple-element.37), channel_id=1, replica_groups=mesh['gx_0'=4,'gx_1'=2,'gy_0'=8,'gy_1'=2,'gz'=2] {'gz'}, use_global_device_ids=true, to_apply=%region_29.30 | all-reduce | flops 2 | bytes 16 | tf_op jit(solution)/shard_map/psum | solution.py:20
  (113 shorter events, 115.9 us)
Async XLA Ops:
  24.5 5.3 %collective-permute-start = (f32[4,16,2,128]{3,1,2,0:T(8,128)S(1)}, f32[4,16,2,128]{3,1,2,0:T(8,128)S(1)}, u32[]{:S(2)}, u32[]{:S(2)}) collective-permute-start(f32[4,16,2,128]{3,1,2,0:T(8,128)S(1)} %get-tuple-element.132), channel_id=1, source_target_pairs={{0,32},{32,64},{64,96},{96,128},{128,160},{160,192},{192,224},{1,3... | collective-permute-start | bytes 196616 | tf_op jit(solution)/shard_map/ppermute | solution.py:31
  28.4 5.0 %collective-permute-start.1 = (f32[4,16,2,128]{3,1,2,0:T(8,128)S(1)}, f32[4,16,2,128]{3,1,2,0:T(8,128)S(1)}, u32[]{:S(2)}, u32[]{:S(2)}) collective-permute-start(f32[4,16,2,128]{3,1,2,0:T(8,128)S(1)} %get-tuple-element.133), channel_id=1, source_target_pairs={{32,0},{64,32},{96,64},{128,96},{160,128},{192,160},{224,192},{33,... | collective-permute-start | bytes 196616 | tf_op jit(solution)/shard_map/ppermute | solution.py:32
  34.2 8.8 %collective-permute-start.2 = (f32[4,16,20,2]{2,1,3,0:T(8,128)S(1)}, f32[4,16,20,2]{2,1,3,0:T(8,128)S(1)}, u32[]{:S(2)}, u32[]{:S(2)}) collective-permute-start(f32[4,16,20,2]{2,1,3,0:T(8,128)S(1)} %copy.202), channel_id=1, source_target_pairs={{0,1},{1,2},{2,3},{3,4},{4,5},{5,6},{6,7},{7,8},{8,9},{9,10},{10,1... | collective-permute-start | bytes 30728 | tf_op jit(solution)/shard_map/ppermute | solution.py:31
  39.2 7.3 %collective-permute-start.3 = (f32[4,16,20,2]{2,1,3,0:T(8,128)S(1)}, f32[4,16,20,2]{2,1,3,0:T(8,128)S(1)}, u32[]{:S(2)}, u32[]{:S(2)}) collective-permute-start(f32[4,16,20,2]{2,1,3,0:T(8,128)S(1)} %copy.203), channel_id=1, source_target_pairs={{1,0},{2,1},{3,2},{4,3},{5,4},{6,5},{7,6},{8,7},{9,8},{10,9},{11,1... | collective-permute-start | bytes 30728 | tf_op jit(solution)/shard_map/ppermute | solution.py:32
  65.2 4.8 %collective-permute-start.4 = (f32[2,8,1,256]{3,2,1,0:T(1,128)S(1)}, f32[2,8,1,256]{3,2,1,0:T(1,128)S(1)}, u32[]{:S(2)}, u32[]{:S(2)}) collective-permute-start(f32[2,8,1,256]{3,2,1,0:T(1,128)S(1)} %get-tuple-element.146), channel_id=1, source_target_pairs={{0,32},{32,64},{64,96},{96,128},{128,160},{160,192},{192,224},{1,3... | collective-permute-start | bytes 49160 | tf_op jit(solution)/shard_map/ppermute | solution.py:31
  68.7 4.5 %collective-permute-start.5 = (f32[2,8,1,256]{3,2,1,0:T(1,128)S(1)}, f32[2,8,1,256]{3,2,1,0:T(1,128)S(1)}, u32[]{:S(2)}, u32[]{:S(2)}) collective-permute-start(f32[2,8,1,256]{3,2,1,0:T(1,128)S(1)} %get-tuple-element.147), channel_id=1, source_target_pairs={{32,0},{64,32},{96,64},{128,96},{160,128},{192,160},{224,192},{33,... | collective-permute-start | bytes 49160 | tf_op jit(solution)/shard_map/ppermute | solution.py:32
  73.4 7.8 %collective-permute-start.6 = (f32[2,8,18,1]{3,2,1,0:T(8,128)S(1)}, f32[2,8,18,1]{3,2,1,0:T(8,128)S(1)}, u32[]{:S(2)}, u32[]{:S(2)}) collective-permute-start(f32[2,8,18,1]{3,2,1,0:T(8,128)S(1)} %get-tuple-element.142), channel_id=1, source_target_pairs={{0,2},{2,4},{4,6},{6,8},{8,10},{10,12},{12,14},{14,16},{16,18},{18... | collective-permute-start | bytes 3464 | tf_op jit(solution)/shard_map/ppermute | solution.py:31
  78.6 7.0 %collective-permute-start.7 = (f32[2,8,18,1]{3,2,1,0:T(8,128)S(1)}, f32[2,8,18,1]{3,2,1,0:T(8,128)S(1)}, u32[]{:S(2)}, u32[]{:S(2)}) collective-permute-start(f32[2,8,18,1]{3,2,1,0:T(8,128)S(1)} %get-tuple-element.143), channel_id=1, source_target_pairs={{2,0},{4,2},{6,4},{8,6},{10,8},{12,10},{14,12},{16,14},{18,16},{20... | collective-permute-start | bytes 3464 | tf_op jit(solution)/shard_map/ppermute | solution.py:32
  85.7 3.8 %collective-permute-start.8 = (f32[2,1,18,258]{3,2,1,0:T(8,128)S(1)}, f32[2,1,18,258]{3,2,1,0:T(8,128)S(1)}, u32[]{:S(2)}, u32[]{:S(2)}) collective-permute-start(f32[2,1,18,258]{3,2,1,0:T(8,128)S(1)} %get-tuple-element.122), channel_id=1, source_target_pairs={{0,1},{2,3},{4,5},{6,7},{8,9},{10,11},{12,13},{14,15},{16,17},{18,... | collective-permute-start | bytes 111464 | tf_op jit(solution)/shard_map/ppermute | solution.py:31
  87.7 6.6 %collective-permute-start.9 = (f32[2,1,18,258]{3,2,1,0:T(8,128)S(1)}, f32[2,1,18,258]{3,2,1,0:T(8,128)S(1)}, u32[]{:S(2)}, u32[]{:S(2)}) collective-permute-start(f32[2,1,18,258]{3,2,1,0:T(8,128)S(1)} %get-tuple-element.123), channel_id=1, source_target_pairs={{1,0},{3,2},{5,4},{7,6},{9,8},{11,10},{13,12},{15,14},{17,16},{19,... | collective-permute-start | bytes 111464 | tf_op jit(solution)/shard_map/ppermute | solution.py:32
  97.4 4.4 %collective-permute-start.10 = (f32[3,8,1,256]{3,2,1,0:T(1,128)S(1)}, f32[3,8,1,256]{3,2,1,0:T(1,128)S(1)}, u32[]{:S(2)}, u32[]{:S(2)}) collective-permute-start(f32[3,8,1,256]{3,2,1,0:T(1,128)S(1)} %get-tuple-element.140), channel_id=1, source_target_pairs={{0,32},{32,64},{64,96},{96,128},{128,160},{160,192},{192,224},{1,3... | collective-permute-start | bytes 73736 | tf_op jit(solution)/shard_map/ppermute | solution.py:31
  100.5 4.6 %collective-permute-start.11 = (f32[3,8,1,256]{3,2,1,0:T(1,128)S(1)}, f32[3,8,1,256]{3,2,1,0:T(1,128)S(1)}, u32[]{:S(2)}, u32[]{:S(2)}) collective-permute-start(f32[3,8,1,256]{3,2,1,0:T(1,128)S(1)} %get-tuple-element.141), channel_id=1, source_target_pairs={{32,0},{64,32},{96,64},{128,96},{160,128},{192,160},{224,192},{33,... | collective-permute-start | bytes 73736 | tf_op jit(solution)/shard_map/ppermute | solution.py:32
  105.3 8.0 %collective-permute-start.12 = (f32[3,8,18,1]{3,2,1,0:T(8,128)S(1)}, f32[3,8,18,1]{3,2,1,0:T(8,128)S(1)}, u32[]{:S(2)}, u32[]{:S(2)}) collective-permute-start(f32[3,8,18,1]{3,2,1,0:T(8,128)S(1)} %get-tuple-element.130), channel_id=1, source_target_pairs={{0,2},{2,4},{4,6},{6,8},{8,10},{10,12},{12,14},{14,16},{16,18},{18... | collective-permute-start | bytes 5192 | tf_op jit(solution)/shard_map/ppermute | solution.py:31
  109.7 8.0 %collective-permute-start.13 = (f32[3,8,18,1]{3,2,1,0:T(8,128)S(1)}, f32[3,8,18,1]{3,2,1,0:T(8,128)S(1)}, u32[]{:S(2)}, u32[]{:S(2)}) collective-permute-start(f32[3,8,18,1]{3,2,1,0:T(8,128)S(1)} %get-tuple-element.131), channel_id=1, source_target_pairs={{2,0},{4,2},{6,4},{8,6},{10,8},{12,10},{14,12},{16,14},{18,16},{20... | collective-permute-start | bytes 5192 | tf_op jit(solution)/shard_map/ppermute | solution.py:32
  117.9 3.7 %collective-permute-start.14 = (f32[3,1,18,258]{3,2,1,0:T(8,128)S(1)}, f32[3,1,18,258]{3,2,1,0:T(8,128)S(1)}, u32[]{:S(2)}, u32[]{:S(2)}) collective-permute-start(f32[3,1,18,258]{3,2,1,0:T(8,128)S(1)} %get-tuple-element.118), channel_id=1, source_target_pairs={{0,1},{2,3},{4,5},{6,7},{8,9},{10,11},{12,13},{14,15},{16,17},{18,... | collective-permute-start | bytes 167192 | tf_op jit(solution)/shard_map/ppermute | solution.py:31
  119.9 7.0 %collective-permute-start.15 = (f32[3,1,18,258]{3,2,1,0:T(8,128)S(1)}, f32[3,1,18,258]{3,2,1,0:T(8,128)S(1)}, u32[]{:S(2)}, u32[]{:S(2)}) collective-permute-start(f32[3,1,18,258]{3,2,1,0:T(8,128)S(1)} %get-tuple-element.119), channel_id=1, source_target_pairs={{1,0},{3,2},{5,4},{7,6},{9,8},{11,10},{13,12},{15,14},{17,16},{19,... | collective-permute-start | bytes 167192 | tf_op jit(solution)/shard_map/ppermute | solution.py:32
  181.9 5.0 %collective-permute-start.16 = (f32[3,8,1,256]{3,2,1,0:T(1,128)S(1)}, f32[3,8,1,256]{3,2,1,0:T(1,128)S(1)}, u32[]{:S(2)}, u32[]{:S(2)}) collective-permute-start(f32[3,8,1,256]{3,2,1,0:T(1,128)S(1)} %get-tuple-element.138), channel_id=1, source_target_pairs={{0,32},{32,64},{64,96},{96,128},{128,160},{160,192},{192,224},{1,3... | collective-permute-start | bytes 73736 | tf_op jit(solution)/shard_map/ppermute | solution.py:31
  185.6 4.6 %collective-permute-start.17 = (f32[3,8,1,256]{3,2,1,0:T(1,128)S(1)}, f32[3,8,1,256]{3,2,1,0:T(1,128)S(1)}, u32[]{:S(2)}, u32[]{:S(2)}) collective-permute-start(f32[3,8,1,256]{3,2,1,0:T(1,128)S(1)} %get-tuple-element.139), channel_id=1, source_target_pairs={{32,0},{64,32},{96,64},{128,96},{160,128},{192,160},{224,192},{33,... | collective-permute-start | bytes 73736 | tf_op jit(solution)/shard_map/ppermute | solution.py:32
  190.4 8.8 %collective-permute-start.18 = (f32[3,8,18,1]{3,2,1,0:T(8,128)S(1)}, f32[3,8,18,1]{3,2,1,0:T(8,128)S(1)}, u32[]{:S(2)}, u32[]{:S(2)}) collective-permute-start(f32[3,8,18,1]{3,2,1,0:T(8,128)S(1)} %get-tuple-element.128), channel_id=1, source_target_pairs={{0,2},{2,4},{4,6},{6,8},{8,10},{10,12},{12,14},{14,16},{16,18},{18... | collective-permute-start | bytes 5192 | tf_op jit(solution)/shard_map/ppermute | solution.py:31
  195.5 8.0 %collective-permute-start.19 = (f32[3,8,18,1]{3,2,1,0:T(8,128)S(1)}, f32[3,8,18,1]{3,2,1,0:T(8,128)S(1)}, u32[]{:S(2)}, u32[]{:S(2)}) collective-permute-start(f32[3,8,18,1]{3,2,1,0:T(8,128)S(1)} %get-tuple-element.129), channel_id=1, source_target_pairs={{2,0},{4,2},{6,4},{8,6},{10,8},{12,10},{14,12},{16,14},{18,16},{20... | collective-permute-start | bytes 5192 | tf_op jit(solution)/shard_map/ppermute | solution.py:32
  203.8 4.0 %collective-permute-start.20 = (f32[3,1,18,258]{3,2,1,0:T(8,128)S(1)}, f32[3,1,18,258]{3,2,1,0:T(8,128)S(1)}, u32[]{:S(2)}, u32[]{:S(2)}) collective-permute-start(f32[3,1,18,258]{3,2,1,0:T(8,128)S(1)} %get-tuple-element.116), channel_id=1, source_target_pairs={{0,1},{2,3},{4,5},{6,7},{8,9},{10,11},{12,13},{14,15},{16,17},{18,... | collective-permute-start | bytes 167192 | tf_op jit(solution)/shard_map/ppermute | solution.py:31
  206.0 7.0 %collective-permute-start.21 = (f32[3,1,18,258]{3,2,1,0:T(8,128)S(1)}, f32[3,1,18,258]{3,2,1,0:T(8,128)S(1)}, u32[]{:S(2)}, u32[]{:S(2)}) collective-permute-start(f32[3,1,18,258]{3,2,1,0:T(8,128)S(1)} %get-tuple-element.117), channel_id=1, source_target_pairs={{1,0},{3,2},{5,4},{7,6},{9,8},{11,10},{13,12},{15,14},{17,16},{19,... | collective-permute-start | bytes 167192 | tf_op jit(solution)/shard_map/ppermute | solution.py:32
  266.1 3.2 collective-permute-start.22
  268.1 5.5 %collective-permute-start.23 = (f32[3,8,1,256]{3,2,1,0:T(1,128)S(1)}, f32[3,8,1,256]{3,2,1,0:T(1,128)S(1)}, u32[]{:S(2)}, u32[]{:S(2)}) collective-permute-start(f32[3,8,1,256]{3,2,1,0:T(1,128)S(1)} %get-tuple-element.137), channel_id=1, source_target_pairs={{32,0},{64,32},{96,64},{128,96},{160,128},{192,160},{224,192},{33,... | collective-permute-start | bytes 73736 | tf_op jit(solution)/shard_map/ppermute | solution.py:32
  273.8 8.6 %collective-permute-start.24 = (f32[3,8,18,1]{3,2,1,0:T(8,128)S(1)}, f32[3,8,18,1]{3,2,1,0:T(8,128)S(1)}, u32[]{:S(2)}, u32[]{:S(2)}) collective-permute-start(f32[3,8,18,1]{3,2,1,0:T(8,128)S(1)} %get-tuple-element.126), channel_id=1, source_target_pairs={{0,2},{2,4},{4,6},{6,8},{8,10},{10,12},{12,14},{14,16},{16,18},{18... | collective-permute-start | bytes 5192 | tf_op jit(solution)/shard_map/ppermute | solution.py:31
  278.8 8.0 %collective-permute-start.25 = (f32[3,8,18,1]{3,2,1,0:T(8,128)S(1)}, f32[3,8,18,1]{3,2,1,0:T(8,128)S(1)}, u32[]{:S(2)}, u32[]{:S(2)}) collective-permute-start(f32[3,8,18,1]{3,2,1,0:T(8,128)S(1)} %get-tuple-element.127), channel_id=1, source_target_pairs={{2,0},{4,2},{6,4},{8,6},{10,8},{12,10},{14,12},{16,14},{18,16},{20... | collective-permute-start | bytes 5192 | tf_op jit(solution)/shard_map/ppermute | solution.py:32
  287.0 3.8 %collective-permute-start.26 = (f32[3,1,18,258]{3,2,1,0:T(8,128)S(1)}, f32[3,1,18,258]{3,2,1,0:T(8,128)S(1)}, u32[]{:S(2)}, u32[]{:S(2)}) collective-permute-start(f32[3,1,18,258]{3,2,1,0:T(8,128)S(1)} %get-tuple-element.114), channel_id=1, source_target_pairs={{0,1},{2,3},{4,5},{6,7},{8,9},{10,11},{12,13},{14,15},{16,17},{18,... | collective-permute-start | bytes 167192 | tf_op jit(solution)/shard_map/ppermute | solution.py:31
  288.8 7.0 %collective-permute-start.27 = (f32[3,1,18,258]{3,2,1,0:T(8,128)S(1)}, f32[3,1,18,258]{3,2,1,0:T(8,128)S(1)}, u32[]{:S(2)}, u32[]{:S(2)}) collective-permute-start(f32[3,1,18,258]{3,2,1,0:T(8,128)S(1)} %get-tuple-element.115), channel_id=1, source_target_pairs={{1,0},{3,2},{5,4},{7,6},{9,8},{11,10},{13,12},{15,14},{17,16},{19,... | collective-permute-start | bytes 167192 | tf_op jit(solution)/shard_map/ppermute | solution.py:32
where the time goes:
time: 351 us; the launch traced here: 350 us
  blocking collectives  140 us (40%)
  starting transfers between devices  71.6 us (20%)
  waiting for transfers between devices  65 us (19%)
  other arithmetic  52.8 us (15%)
  between operations  11.2 us (3%)
  local copies, waits for them, and re-layouts  9.35 us (3%)
    psum x15, blocking collectives, over_axes(): value = lax.psum(value, axis)  127 us
    ppermute x14, waiting for transfers between devices, padded(): after = lax.ppermute(initial, axis, down)  58.5 us
    ppermute x14, starting transfers between devices, padded(): before = lax.ppermute(last, axis, up)  48.3 us
    ppermute x14, starting transfers between devices, padded(): after = lax.ppermute(initial, axis, down)  23.3 us
    another operation x9, other arithmetic, apply_operator(): return jnp.stack(parts)  19.1 us
    another operation x2, other arithmetic, per_device(): jnp.stack([starting_kelvin, diffusive_coefficient, power, inverse_cap])  16.4 us
    all_to_all x1, blocking collectives, per_device(): lax.all_to_all(fields, 'gz', split_axis=1, concat_axis=3, tiled=True)  12.7 us
  transfers between devices with their start and end apart: 28, of which 20 were waited for; matrix products, arithmetic and copies ran while one was open for 1% of the time, Pallas kernels for 0%

commit v1 on v0

--- a/solution.py
+++ b/solution.py
@@ -15,9 +15,14 @@
 strain_gain = 2.0
 
 
+def set_figure(x_part, which_axis):
+    o_now = lax.all_gather(x_part, axis_name=which_axis).sum(axis=0)
+    return o_now
+
+
 def over_axes(value, axes):
     for axis in axes:
-        value = lax.psum(value, axis)
+        value = set_figure(value, which_axis=axis)
     return value
 
 

time: 351 us -> 404 us (1.15)
  local copies, waits for them, and re-layouts: 9.35 us -> 53.7 us
  waiting for transfers between devices: 65 us -> 28 us
  starting transfers between devices: 71.6 us -> 95.3 us
  other arithmetic: 52.8 us -> 71.4 us
    unnamed x0 -> x15, blocking collectives: none -> 135 us
    psum x15 -> x0, blocking collectives: 127 us -> none  [over_axes(): value = lax.psum(value, axis)]
    ppermute x14, waiting for transfers between devices: 58.5 us -> 8.83 us  [padded(): after = lax.ppermute(initial, axis, down)]
    unnamed x1 -> x76, local copies, waits for them, and re-layouts: 0.7 us -> 45 us
    reduce_sum x0 -> x30, other arithmetic: none -> 18.5 us  [set_figure(): o_now = lax.all_gather(x_part, axis_name=which_axis).sum(axis=0)]
    ppermute x14, waiting for transfers between devices: 6.53 us -> 19.2 us  [padded(): before = lax.ppermute(last, axis, up)]
    ppermute x14, starting transfers between devices: 23.3 us -> 35.3 us  [padded(): after = lax.ppermute(initial, axis, down)]
    ppermute x14, starting transfers between devices: 48.3 us -> 60 us  [padded(): before = lax.ppermute(last, axis, up)]
  transfers between devices with their start and end apart: 28 -> 28, of which waited for: 20 -> 18; matrix products, arithmetic and copies ran while one was open for 1% -> 1% of each run, Pallas kernels for 0% -> 0%
where the time goes in v1:
time: 404 us; the launch traced here: 402 us
  blocking collectives  143 us (35%)
  starting transfers between devices  95.3 us (24%)
  other arithmetic  71.4 us (18%)
  local copies, waits for them, and re-layouts  53.7 us (13%)
  waiting for transfers between devices  28 us (7%)
  between operations  11.1 us (3%)
    unnamed x15, blocking collectives  135 us
    ppermute x14, starting transfers between devices, padded(): before = lax.ppermute(last, axis, up)  60 us
    unnamed x76, local copies, waits for them, and re-layouts  45 us
    ppermute x14, starting transfers between devices, padded(): after = lax.ppermute(initial, axis, down)  35.3 us
    ppermute x14, waiting for transfers between devices, padded(): before = lax.ppermute(last, axis, up)  19.2 us
    another operation x9, other arithmetic, apply_operator(): return jnp.stack(parts)  19.1 us
    reduce_sum x30, other arithmetic, set_figure(): o_now = lax.all_gather(x_part, axis_name=which_axis).sum(axis=0)  18.5 us
    another operation x2, other arithmetic, per_device(): jnp.stack([starting_kelvin, diffusive_coefficient, power, inverse_cap])  16.3 us
  transfers between devices with their start and end apart: 28, of which 18 were waited for; matrix products, arithmetic and copies ran while one was open for 1% of the time, Pallas kernels for 0%

profile of v1, /device:TPU:1, one launch (start us, length us, event | category | flops | bytes accessed | tf_op | source)
XLA Modules:
  0.0 402.0 jit_solution(13412739810825296999)
XLA Ops:
  8.1 5.1 %add_bitcast_fusion.11 = (f32[1,16,16,128]{3,1,2,0:T(8,128)S(1)}, f32[1,16,16,128]{3,1,2,0:T(8,128)S(1)}) fusion(pred[16,16,128]{2,0,1:T(8,128)(4,1)S(1)} %get-tuple-element.98, pred[16,16,128]{2,0,1:T(8,128)(4,1)S(1)} %get-tuple-element.97, pred[16,16,128]{2,0,1:T(8,128)(4,1)S(1)} %get-tuple-element.96, pred[16,16,128]{2,0,1:T(8,128)(4,1)S(1)} %get-tuple-element.95, ...), kind=kLoop, calls=%fused_computation.621 | loop fusion | flops 491520 | bytes 393248 | tf_op jit(solution)/shard_map/stack | solution.py:146
  13.2 11.2 %copy_bitcast_fusion = (f32[1,16,16,128]{3,1,2,0:T(8,128)S(1)}, f32[1,16,16,128]{3,1,2,0:T(8,128)S(1)}) fusion(f32[16,16,128]{2,1,0:T(8,128)} %param.5, f32[]{:T(128)} %bitcast.21, f32[]{:T(128)} %bitcast.20, f32[]{:T(128)} %bitcast.19, f32[]{:T(128)} %bitcast.18, f32[]{:T(128)} %bitcast.17, f32[]{:T(128)} %bitcast.16, f32[]{:T(128)} %bitcast.15, ...), kind=kLoop, calls=%fused_computation.521 | loop fusion | flops 1540096 | bytes 524352 | tf_op jit(solution)/shard_map/stack | solution.py:146
  25.7 4.6 %collective-permute-start = (f32[4,16,2,128]{3,1,2,0:T(8,128)S(1)}, f32[4,16,2,128]{3,1,2,0:T(8,128)S(1)}, u32[]{:S(2)}, u32[]{:S(2)}) collective-permute-start(f32[4,16,2,128]{3,1,2,0:T(8,128)S(1)} %get-tuple-element.132), channel_id=1, source_target_pairs={{0,32},{32,64},{64,96},{96,128},{128,160},{160,192},{192,224},{1,3... | collective-permute-start | bytes 196616 | tf_op jit(solution)/shard_map/ppermute | solution.py:36
  32.4 6.6 %collective-permute-start.3 = (f32[4,16,20,2]{2,1,3,0:T(8,128)S(1)}, f32[4,16,20,2]{2,1,3,0:T(8,128)S(1)}, u32[]{:S(2)}, u32[]{:S(2)}) collective-permute-start(f32[4,16,20,2]{2,1,3,0:T(8,128)S(1)} %copy.203), channel_id=1, source_target_pairs={{1,0},{2,1},{3,2},{4,3},{5,4},{6,5},{7,6},{8,7},{9,8},{10,9},{11,1... | collective-permute-start | bytes 30728 | tf_op jit(solution)/shard_map/ppermute | solution.py:37
  41.9 4.6 %collective-permute-done.2 = f32[4,16,20,2]{2,1,3,0:T(8,128)S(1)} collective-permute-done((f32[4,16,20,2]{2,1,3,0:T(8,128)S(1)}, f32[4,16,20,2]{2,1,3,0:T(8,128)S(1)}, u32[]{:S(2)}, u32[]{:S(2)}) %collective-permute-start.2) | collective-permute-done | bytes 10272 | tf_op jit(solution)/shard_map/ppermute | solution.py:36
  52.2 7.9 %all_to_all.18 = f32[2,16,16,128]{3,2,0,1:T(8,128)S(1)} all-to-all(f32[2,16,16,128]{3,2,0,1:T(8,128)S(1)} %copy.206), channel_id=1, replica_groups=mesh['gx_0'=4,'gx_1'=2,'gy_0'=8,'gy_1'=2,'gz'=2] {'gz'}, dimensions={1} | all-to-all | bytes 524288 | tf_op jit(solution)/shard_map/all_to_all | solution.py:161
  61.8 4.0 collective-permute-start.4
  66.9 6.4 %collective-permute-start.7 = (f32[2,8,18,1]{3,2,1,0:T(8,128)S(1)}, f32[2,8,18,1]{3,2,1,0:T(8,128)S(1)}, u32[]{:S(2)}, u32[]{:S(2)}) collective-permute-start(f32[2,8,18,1]{3,2,1,0:T(8,128)S(1)} %get-tuple-element.143), channel_id=1, source_target_pairs={{2,0},{4,2},{6,4},{8,6},{10,8},{12,10},{14,12},{16,14},{18,16},{20... | collective-permute-start | bytes 3464 | tf_op jit(solution)/shard_map/ppermute | solution.py:37
  79.5 5.5 %collective-permute-start.8 = (f32[2,1,18,258]{3,2,1,0:T(8,128)S(1)}, f32[2,1,18,258]{3,2,1,0:T(8,128)S(1)}, u32[]{:S(2)}, u32[]{:S(2)}) collective-permute-start(f32[2,1,18,258]{3,2,1,0:T(8,128)S(1)} %get-tuple-element.122), channel_id=1, source_target_pairs={{0,1},{2,3},{4,5},{6,7},{8,9},{10,11},{12,13},{14,15},{16,17},{18,... | collective-permute-start | bytes 111464 | tf_op jit(solution)/shard_map/ppermute | solution.py:36
  90.9 5.5 %collective-permute-start.10 = (f32[3,8,1,256]{3,2,1,0:T(1,128)S(1)}, f32[3,8,1,256]{3,2,1,0:T(1,128)S(1)}, u32[]{:S(2)}, u32[]{:S(2)}) collective-permute-start(f32[3,8,1,256]{3,2,1,0:T(1,128)S(1)} %get-tuple-element.140), channel_id=1, source_target_pairs={{0,32},{32,64},{64,96},{96,128},{128,160},{160,192},{192,224},{1,3... | collective-permute-start | bytes 73736 | tf_op jit(solution)/shard_map/ppermute | solution.py:36
  99.7 6.1 %collective-permute-start.12 = (f32[3,8,18,1]{3,2,1,0:T(8,128)S(1)}, f32[3,8,18,1]{3,2,1,0:T(8,128)S(1)}, u32[]{:S(2)}, u32[]{:S(2)}) collective-permute-start(f32[3,8,18,1]{3,2,1,0:T(8,128)S(1)} %get-tuple-element.130), channel_id=1, source_target_pairs={{0,2},{2,4},{4,6},{6,8},{8,10},{10,12},{12,14},{14,16},{16,18},{18... | collective-permute-start | bytes 5192 | tf_op jit(solution)/shard_map/ppermute | solution.py:36
  111.0 6.3 %collective-permute-start.14 = (f32[3,1,18,258]{3,2,1,0:T(8,128)S(1)}, f32[3,1,18,258]{3,2,1,0:T(8,128)S(1)}, u32[]{:S(2)}, u32[]{:S(2)}) collective-permute-start(f32[3,1,18,258]{3,2,1,0:T(8,128)S(1)} %get-tuple-element.118), channel_id=1, source_target_pairs={{0,1},{2,3},{4,5},{6,7},{8,9},{10,11},{12,13},{14,15},{16,17},{18,... | collective-permute-start | bytes 167192 | tf_op jit(solution)/shard_map/ppermute | solution.py:36
  131.3 13.3 %all-reduce.39 = (f32[4]{0:T(128)S(1)}, f32[4]{0:T(128)S(1)}) all-reduce(f32[4]{0:T(128)S(1)} %dynamic-update-slice, f32[4]{0:T(128)S(1)} %dynamic-update-slice.5), channel_id=1, replica_groups=mesh['gx_0'=4,'gx_1'=2,'gy_0'=8,'gy_1'=2,'gz'=2] {'gx_0'}, use_global_device_ids=true, to_apply=%add.4 | all-reduce | flops 8 | bytes 64
  157.8 16.1 %all-reduce.36 = (f32[8]{0:T(128)S(1)}, f32[8]{0:T(128)S(1)}) all-reduce(f32[8]{0:T(128)S(1)} %dynamic-update-slice.2, f32[8]{0:T(128)S(1)} %dynamic-update-slice.7), channel_id=1, replica_groups=mesh['gx_0'=4,'gx_1'=2,'gy_0'=8,'gy_1'=2,'gz'=2] {'gy_0'}, use_global_device_ids=true, to_apply=%add.6 | all-reduce | flops 16 | bytes 128
  178.4 11.0 %all-reduce.45 = (f32[2]{0:T(128)S(1)}, f32[2]{0:T(128)S(1)}) all-reduce(f32[2]{0:T(128)S(1)} %dynamic-update-slice.3, f32[2]{0:T(128)S(1)} %dynamic-update-slice.8), channel_id=1, replica_groups=mesh['gx_0'=4,'gx_1'=2,'gy_0'=8,'gy_1'=2,'gz'=2] {'gy_1'}, use_global_device_ids=true, to_apply=%add.7 | all-reduce | flops 4 | bytes 32
  193.4 5.9 %all-reduce.42 = (f32[2]{0:T(128)S(1)}, f32[2]{0:T(128)S(1)}) all-reduce(f32[2]{0:T(128)S(1)} %dynamic-update-slice.4, f32[2]{0:T(128)S(1)} %dynamic-update-slice.9), channel_id=1, replica_groups=mesh['gx_0'=4,'gx_1'=2,'gy_0'=8,'gy_1'=2,'gz'=2] {'gz'}, use_global_device_ids=true, to_apply=%add.8 | all-reduce | flops 4 | bytes 32
  203.3 4.0 collective-permute-start.16
  208.5 4.3 %collective-permute-start.19 = (f32[3,8,18,1]{3,2,1,0:T(8,128)S(1)}, f32[3,8,18,1]{3,2,1,0:T(8,128)S(1)}, u32[]{:S(2)}, u32[]{:S(2)}) collective-permute-start(f32[3,8,18,1]{3,2,1,0:T(8,128)S(1)} %get-tuple-element.129), channel_id=1, source_target_pairs={{2,0},{4,2},{6,4},{8,6},{10,8},{12,10},{14,12},{16,14},{18,16},{20... | collective-permute-start | bytes 5192 | tf_op jit(solution)/shard_map/ppermute | solution.py:37
  220.5 5.7 %collective-permute-start.20 = (f32[3,1,18,258]{3,2,1,0:T(8,128)S(1)}, f32[3,1,18,258]{3,2,1,0:T(8,128)S(1)}, u32[]{:S(2)}, u32[]{:S(2)}) collective-permute-start(f32[3,1,18,258]{3,2,1,0:T(8,128)S(1)} %get-tuple-element.116), channel_id=1, source_target_pairs={{0,1},{2,3},{4,5},{6,7},{8,9},{10,11},{12,13},{14,15},{16,17},{18,... | collective-permute-start | bytes 167192 | tf_op jit(solution)/shard_map/ppermute | solution.py:36
  237.7 8.4 %all-reduce.38 = (f32[4]{0:T(128)S(1)}, f32[4]{0:T(128)S(1)}) all-reduce(f32[4]{0:T(128)S(1)} %dynamic-update-slice.10, f32[4]{0:T(128)S(1)} %dynamic-update-slice.15), channel_id=1, replica_groups=mesh['gx_0'=4,'gx_1'=2,'gy_0'=8,'gy_1'=2,'gz'=2] {'gx_0'}, use_global_device_ids=true, to_apply=%add.14 | all-reduce | flops 8 | bytes 64
  250.1 3.8 all-reduce.47
  257.9 12.2 %all-reduce.35 = (f32[8]{0:T(128)S(1)}, f32[8]{0:T(128)S(1)}) all-reduce(f32[8]{0:T(128)S(1)} %dynamic-update-slice.12, f32[8]{0:T(128)S(1)} %dynamic-update-slice.17), channel_id=1, replica_groups=mesh['gx_0'=4,'gx_1'=2,'gy_0'=8,'gy_1'=2,'gz'=2] {'gy_0'}, use_global_device_ids=true, to_apply=%add.16 | all-reduce | flops 16 | bytes 128
  273.9 12.1 %all-reduce.44 = (f32[2]{0:T(128)S(1)}, f32[2]{0:T(128)S(1)}) all-reduce(f32[2]{0:T(128)S(1)} %dynamic-update-slice.13, f32[2]{0:T(128)S(1)} %dynamic-update-slice.18), channel_id=1, replica_groups=mesh['gx_0'=4,'gx_1'=2,'gy_0'=8,'gy_1'=2,'gz'=2] {'gy_1'}, use_global_device_ids=true, to_apply=%add.17 | all-reduce | flops 4 | bytes 32
  290.0 5.9 %all-reduce.41 = (f32[2]{0:T(128)S(1)}, f32[2]{0:T(128)S(1)}) all-reduce(f32[2]{0:T(128)S(1)} %dynamic-update-slice.14, f32[2]{0:T(128)S(1)} %dynamic-update-slice.19), channel_id=1, replica_groups=mesh['gx_0'=4,'gx_1'=2,'gy_0'=8,'gy_1'=2,'gz'=2] {'gz'}, use_global_device_ids=true, to_apply=%add.18 | all-reduce | flops 4 | bytes 32
  303.2 4.0 collective-permute-start.22
  308.3 4.3 %collective-permute-start.25 = (f32[3,8,18,1]{3,2,1,0:T(8,128)S(1)}, f32[3,8,18,1]{3,2,1,0:T(8,128)S(1)}, u32[]{:S(2)}, u32[]{:S(2)}) collective-permute-start(f32[3,8,18,1]{3,2,1,0:T(8,128)S(1)} %get-tuple-element.127), channel_id=1, source_target_pairs={{2,0},{4,2},{6,4},{8,6},{10,8},{12,10},{14,12},{16,14},{18,16},{20... | collective-permute-start | bytes 5192 | tf_op jit(solution)/shard_map/ppermute | solution.py:37
  319.6 5.8 %collective-permute-start.26 = (f32[3,1,18,258]{3,2,1,0:T(8,128)S(1)}, f32[3,1,18,258]{3,2,1,0:T(8,128)S(1)}, u32[]{:S(2)}, u32[]{:S(2)}) collective-permute-start(f32[3,1,18,258]{3,2,1,0:T(8,128)S(1)} %get-tuple-element.114), channel_id=1, source_target_pairs={{0,1},{2,3},{4,5},{6,7},{8,9},{10,11},{12,13},{14,15},{16,17},{18,... | collective-permute-start | bytes 167192 | tf_op jit(solution)/shard_map/ppermute | solution.py:36
  337.0 8.5 %all-reduce.37 = (f32[4]{0:T(128)S(1)}, f32[4]{0:T(128)S(1)}) all-reduce(f32[4]{0:T(128)S(1)} %dynamic-update-slice.20, f32[4]{0:T(128)S(1)} %dynamic-update-slice.25), channel_id=1, replica_groups=mesh['gx_0'=4,'gx_1'=2,'gy_0'=8,'gy_1'=2,'gz'=2] {'gx_0'}, use_global_device_ids=true, to_apply=%add.24 | all-reduce | flops 8 | bytes 64
  349.5 3.8 all-reduce.46
  357.4 12.0 %all-reduce.34 = (f32[8]{0:T(128)S(1)}, f32[8]{0:T(128)S(1)}) all-reduce(f32[8]{0:T(128)S(1)} %dynamic-update-slice.22, f32[8]{0:T(128)S(1)} %dynamic-update-slice.27), channel_id=1, replica_groups=mesh['gx_0'=4,'gx_1'=2,'gy_0'=8,'gy_1'=2,'gz'=2] {'gy_0'}, use_global_device_ids=true, to_apply=%add.26 | all-reduce | flops 16 | bytes 128
  373.2 12.0 %all-reduce.43 = (f32[2]{0:T(128)S(1)}, f32[2]{0:T(128)S(1)}) all-reduce(f32[2]{0:T(128)S(1)} %dynamic-update-slice.23, f32[2]{0:T(128)S(1)} %dynamic-update-slice.28), channel_id=1, replica_groups=mesh['gx_0'=4,'gx_1'=2,'gy_0'=8,'gy_1'=2,'gz'=2] {'gy_1'}, use_global_device_ids=true, to_apply=%add.27 | all-reduce | flops 4 | bytes 32
  389.9 5.9 %all-reduce.40 = (f32[2]{0:T(128)S(1)}, f32[2]{0:T(128)S(1)}) all-reduce(f32[2]{0:T(128)S(1)} %dynamic-update-slice.24, f32[2]{0:T(128)S(1)} %dynamic-update-slice.29), channel_id=1, replica_groups=mesh['gx_0'=4,'gx_1'=2,'gy_0'=8,'gy_1'=2,'gz'=2] {'gz'}, use_global_device_ids=true, to_apply=%add.28 | all-reduce | flops 4 | bytes 32
  (218 shorter events, 158.3 us)
Async XLA Ops:
  24.4 5.9 %collective-permute-start.1 = (f32[4,16,2,128]{3,1,2,0:T(8,128)S(1)}, f32[4,16,2,128]{3,1,2,0:T(8,128)S(1)}, u32[]{:S(2)}, u32[]{:S(2)}) collective-permute-start(f32[4,16,2,128]{3,1,2,0:T(8,128)S(1)} %get-tuple-element.133), channel_id=1, source_target_pairs={{32,0},{64,32},{96,64},{128,96},{160,128},{192,160},{224,192},{33,... | collective-permute-start | bytes 196616 | tf_op jit(solution)/shard_map/ppermute | solution.py:37
  25.7 5.9 %collective-permute-start = (f32[4,16,2,128]{3,1,2,0:T(8,128)S(1)}, f32[4,16,2,128]{3,1,2,0:T(8,128)S(1)}, u32[]{:S(2)}, u32[]{:S(2)}) collective-permute-start(f32[4,16,2,128]{3,1,2,0:T(8,128)S(1)} %get-tuple-element.132), channel_id=1, source_target_pairs={{0,32},{32,64},{64,96},{96,128},{128,160},{160,192},{192,224},{1,3... | collective-permute-start | bytes 196616 | tf_op jit(solution)/shard_map/ppermute | solution.py:36
  32.4 9.0 %collective-permute-start.3 = (f32[4,16,20,2]{2,1,3,0:T(8,128)S(1)}, f32[4,16,20,2]{2,1,3,0:T(8,128)S(1)}, u32[]{:S(2)}, u32[]{:S(2)}) collective-permute-start(f32[4,16,20,2]{2,1,3,0:T(8,128)S(1)} %copy.203), channel_id=1, source_target_pairs={{1,0},{2,1},{3,2},{4,3},{5,4},{6,5},{7,6},{8,7},{9,8},{10,9},{11,1... | collective-permute-start | bytes 30728 | tf_op jit(solution)/shard_map/ppermute | solution.py:37
  39.5 7.1 %collective-permute-start.2 = (f32[4,16,20,2]{2,1,3,0:T(8,128)S(1)}, f32[4,16,20,2]{2,1,3,0:T(8,128)S(1)}, u32[]{:S(2)}, u32[]{:S(2)}) collective-permute-start(f32[4,16,20,2]{2,1,3,0:T(8,128)S(1)} %copy.202), channel_id=1, source_target_pairs={{0,1},{1,2},{2,3},{3,4},{4,5},{5,6},{6,7},{7,8},{8,9},{9,10},{10,1... | collective-permute-start | bytes 30728 | tf_op jit(solution)/shard_map/ppermute | solution.py:36
  60.5 5.3 %collective-permute-start.5 = (f32[2,8,1,256]{3,2,1,0:T(1,128)S(1)}, f32[2,8,1,256]{3,2,1,0:T(1,128)S(1)}, u32[]{:S(2)}, u32[]{:S(2)}) collective-permute-start(f32[2,8,1,256]{3,2,1,0:T(1,128)S(1)} %get-tuple-element.147), channel_id=1, source_target_pairs={{32,0},{64,32},{96,64},{128,96},{160,128},{192,160},{224,192},{33,... | collective-permute-start | bytes 49160 | tf_op jit(solution)/shard_map/ppermute | solution.py:37
  61.8 4.9 %collective-permute-start.4 = (f32[2,8,1,256]{3,2,1,0:T(1,128)S(1)}, f32[2,8,1,256]{3,2,1,0:T(1,128)S(1)}, u32[]{:S(2)}, u32[]{:S(2)}) collective-permute-start(f32[2,8,1,256]{3,2,1,0:T(1,128)S(1)} %get-tuple-element.146), channel_id=1, source_target_pairs={{0,32},{32,64},{64,96},{96,128},{128,160},{160,192},{192,224},{1,3... | collective-permute-start | bytes 49160 | tf_op jit(solution)/shard_map/ppermute | solution.py:36
  66.9 10.0 %collective-permute-start.7 = (f32[2,8,18,1]{3,2,1,0:T(8,128)S(1)}, f32[2,8,18,1]{3,2,1,0:T(8,128)S(1)}, u32[]{:S(2)}, u32[]{:S(2)}) collective-permute-start(f32[2,8,18,1]{3,2,1,0:T(8,128)S(1)} %get-tuple-element.143), channel_id=1, source_target_pairs={{2,0},{4,2},{6,4},{8,6},{10,8},{12,10},{14,12},{16,14},{18,16},{20... | collective-permute-start | bytes 3464 | tf_op jit(solution)/shard_map/ppermute | solution.py:37
  73.3 4.8 %collective-permute-start.6 = (f32[2,8,18,1]{3,2,1,0:T(8,128)S(1)}, f32[2,8,18,1]{3,2,1,0:T(8,128)S(1)}, u32[]{:S(2)}, u32[]{:S(2)}) collective-permute-start(f32[2,8,18,1]{3,2,1,0:T(8,128)S(1)} %get-tuple-element.142), channel_id=1, source_target_pairs={{0,2},{2,4},{4,6},{6,8},{8,10},{10,12},{12,14},{14,16},{16,18},{18... | collective-permute-start | bytes 3464 | tf_op jit(solution)/shard_map/ppermute | solution.py:36
  78.2 7.3 %collective-permute-start.9 = (f32[2,1,18,258]{3,2,1,0:T(8,128)S(1)}, f32[2,1,18,258]{3,2,1,0:T(8,128)S(1)}, u32[]{:S(2)}, u32[]{:S(2)}) collective-permute-start(f32[2,1,18,258]{3,2,1,0:T(8,128)S(1)} %get-tuple-element.123), channel_id=1, source_target_pairs={{1,0},{3,2},{5,4},{7,6},{9,8},{11,10},{13,12},{15,14},{17,16},{19,... | collective-permute-start | bytes 111464 | tf_op jit(solution)/shard_map/ppermute | solution.py:37
  79.5 7.0 %collective-permute-start.8 = (f32[2,1,18,258]{3,2,1,0:T(8,128)S(1)}, f32[2,1,18,258]{3,2,1,0:T(8,128)S(1)}, u32[]{:S(2)}, u32[]{:S(2)}) collective-permute-start(f32[2,1,18,258]{3,2,1,0:T(8,128)S(1)} %get-tuple-element.122), channel_id=1, source_target_pairs={{0,1},{2,3},{4,5},{6,7},{8,9},{10,11},{12,13},{14,15},{16,17},{18,... | collective-permute-start | bytes 111464 | tf_op jit(solution)/shard_map/ppermute | solution.py:36
  89.6 6.8 %collective-permute-start.11 = (f32[3,8,1,256]{3,2,1,0:T(1,128)S(1)}, f32[3,8,1,256]{3,2,1,0:T(1,128)S(1)}, u32[]{:S(2)}, u32[]{:S(2)}) collective-permute-start(f32[3,8,1,256]{3,2,1,0:T(1,128)S(1)} %get-tuple-element.141), channel_id=1, source_target_pairs={{32,0},{64,32},{96,64},{128,96},{160,128},{192,160},{224,192},{33,... | collective-permute-start | bytes 73736 | tf_op jit(solution)/shard_map/ppermute | solution.py:37
  90.9 6.4 %collective-permute-start.10 = (f32[3,8,1,256]{3,2,1,0:T(1,128)S(1)}, f32[3,8,1,256]{3,2,1,0:T(1,128)S(1)}, u32[]{:S(2)}, u32[]{:S(2)}) collective-permute-start(f32[3,8,1,256]{3,2,1,0:T(1,128)S(1)} %get-tuple-element.140), channel_id=1, source_target_pairs={{0,32},{32,64},{64,96},{96,128},{128,160},{160,192},{192,224},{1,3... | collective-permute-start | bytes 73736 | tf_op jit(solution)/shard_map/ppermute | solution.py:36
  97.4 19.9 %copy-start.4 = (u32[256]{0:T(256)S(1)}, u32[256]{0:T(256)}, u32[]{:S(2)}) copy-start(u32[256]{0:T(256)} %constant.220) | copy-start | bytes 3076
  97.5 10.8 %collective-permute-start.13 = (f32[3,8,18,1]{3,2,1,0:T(8,128)S(1)}, f32[3,8,18,1]{3,2,1,0:T(8,128)S(1)}, u32[]{:S(2)}, u32[]{:S(2)}) collective-permute-start(f32[3,8,18,1]{3,2,1,0:T(8,128)S(1)} %get-tuple-element.131), channel_id=1, source_target_pairs={{2,0},{4,2},{6,4},{8,6},{10,8},{12,10},{14,12},{16,14},{18,16},{20... | collective-permute-start | bytes 5192 | tf_op jit(solution)/shard_map/ppermute | solution.py:37
  99.7 9.8 %collective-permute-start.12 = (f32[3,8,18,1]{3,2,1,0:T(8,128)S(1)}, f32[3,8,18,1]{3,2,1,0:T(8,128)S(1)}, u32[]{:S(2)}, u32[]{:S(2)}) collective-permute-start(f32[3,8,18,1]{3,2,1,0:T(8,128)S(1)} %get-tuple-element.130), channel_id=1, source_target_pairs={{0,2},{2,4},{4,6},{6,8},{8,10},{10,12},{12,14},{14,16},{16,18},{18... | collective-permute-start | bytes 5192 | tf_op jit(solution)/shard_map/ppermute | solution.py:36
  109.7 8.2 %collective-permute-start.15 = (f32[3,1,18,258]{3,2,1,0:T(8,128)S(1)}, f32[3,1,18,258]{3,2,1,0:T(8,128)S(1)}, u32[]{:S(2)}, u32[]{:S(2)}) collective-permute-start(f32[3,1,18,258]{3,2,1,0:T(8,128)S(1)} %get-tuple-element.119), channel_id=1, source_target_pairs={{1,0},{3,2},{5,4},{7,6},{9,8},{11,10},{13,12},{15,14},{17,16},{19,... | collective-permute-start | bytes 167192 | tf_op jit(solution)/shard_map/ppermute | solution.py:37
  111.0 7.9 %collective-permute-start.14 = (f32[3,1,18,258]{3,2,1,0:T(8,128)S(1)}, f32[3,1,18,258]{3,2,1,0:T(8,128)S(1)}, u32[]{:S(2)}, u32[]{:S(2)}) collective-permute-start(f32[3,1,18,258]{3,2,1,0:T(8,128)S(1)} %get-tuple-element.118), channel_id=1, source_target_pairs={{0,1},{2,3},{4,5},{6,7},{8,9},{10,11},{12,13},{14,15},{16,17},{18,... | collective-permute-start | bytes 167192 | tf_op jit(solution)/shard_map/ppermute | solution.py:36
  124.6 24.2 %copy-start.2 = (u32[256]{0:T(256)S(1)}, u32[256]{0:T(256)}, u32[]{:S(2)}) copy-start(u32[256]{0:T(256)} %constant.230) | copy-start | bytes 3076
  124.6 32.6 %copy-start.1 = (u32[256]{0:T(256)S(1)}, u32[256]{0:T(256)}, u32[]{:S(2)}) copy-start(u32[256]{0:T(256)} %constant.235) | copy-start | bytes 3076
  124.6 53.1 %copy-start = (u32[256]{0:T(256)S(1)}, u32[256]{0:T(256)}, u32[]{:S(2)}) copy-start(u32[256]{0:T(256)} %constant.240) | copy-start | bytes 3076
  202.0 5.3 %collective-permute-start.17 = (f32[3,8,1,256]{3,2,1,0:T(1,128)S(1)}, f32[3,8,1,256]{3,2,1,0:T(1,128)S(1)}, u32[]{:S(2)}, u32[]{:S(2)}) collective-permute-start(f32[3,8,1,256]{3,2,1,0:T(1,128)S(1)} %get-tuple-element.139), channel_id=1, source_target_pairs={{32,0},{64,32},{96,64},{128,96},{160,128},{192,160},{224,192},{33,... | collective-permute-start | bytes 73736 | tf_op jit(solution)/shard_map/ppermute | solution.py:37
  203.3 4.9 %collective-permute-start.16 = (f32[3,8,1,256]{3,2,1,0:T(1,128)S(1)}, f32[3,8,1,256]{3,2,1,0:T(1,128)S(1)}, u32[]{:S(2)}, u32[]{:S(2)}) collective-permute-start(f32[3,8,1,256]{3,2,1,0:T(1,128)S(1)} %get-tuple-element.138), channel_id=1, source_target_pairs={{0,32},{32,64},{64,96},{96,128},{128,160},{160,192},{192,224},{1,3... | collective-permute-start | bytes 73736 | tf_op jit(solution)/shard_map/ppermute | solution.py:36
  208.5 9.3 %collective-permute-start.19 = (f32[3,8,18,1]{3,2,1,0:T(8,128)S(1)}, f32[3,8,18,1]{3,2,1,0:T(8,128)S(1)}, u32[]{:S(2)}, u32[]{:S(2)}) collective-permute-start(f32[3,8,18,1]{3,2,1,0:T(8,128)S(1)} %get-tuple-element.129), channel_id=1, source_target_pairs={{2,0},{4,2},{6,4},{8,6},{10,8},{12,10},{14,12},{16,14},{18,16},{20... | collective-permute-start | bytes 5192 | tf_op jit(solution)/shard_map/ppermute | solution.py:37
  212.7 6.3 %collective-permute-start.18 = (f32[3,8,18,1]{3,2,1,0:T(8,128)S(1)}, f32[3,8,18,1]{3,2,1,0:T(8,128)S(1)}, u32[]{:S(2)}, u32[]{:S(2)}) collective-permute-start(f32[3,8,18,1]{3,2,1,0:T(8,128)S(1)} %get-tuple-element.128), channel_id=1, source_target_pairs={{0,2},{2,4},{4,6},{6,8},{8,10},{10,12},{12,14},{14,16},{16,18},{18... | collective-permute-start | bytes 5192 | tf_op jit(solution)/shard_map/ppermute | solution.py:36
  219.2 7.0 %collective-permute-start.21 = (f32[3,1,18,258]{3,2,1,0:T(8,128)S(1)}, f32[3,1,18,258]{3,2,1,0:T(8,128)S(1)}, u32[]{:S(2)}, u32[]{:S(2)}) collective-permute-start(f32[3,1,18,258]{3,2,1,0:T(8,128)S(1)} %get-tuple-element.117), channel_id=1, source_target_pairs={{1,0},{3,2},{5,4},{7,6},{9,8},{11,10},{13,12},{15,14},{17,16},{19,... | collective-permute-start | bytes 167192 | tf_op jit(solution)/shard_map/ppermute | solution.py:37
  220.5 7.2 %collective-permute-start.20 = (f32[3,1,18,258]{3,2,1,0:T(8,128)S(1)}, f32[3,1,18,258]{3,2,1,0:T(8,128)S(1)}, u32[]{:S(2)}, u32[]{:S(2)}) collective-permute-start(f32[3,1,18,258]{3,2,1,0:T(8,128)S(1)} %get-tuple-element.116), channel_id=1, source_target_pairs={{0,1},{2,3},{4,5},{6,7},{8,9},{10,11},{12,13},{14,15},{16,17},{18,... | collective-permute-start | bytes 167192 | tf_op jit(solution)/shard_map/ppermute | solution.py:36
  301.9 5.3 %collective-permute-start.23 = (f32[3,8,1,256]{3,2,1,0:T(1,128)S(1)}, f32[3,8,1,256]{3,2,1,0:T(1,128)S(1)}, u32[]{:S(2)}, u32[]{:S(2)}) collective-permute-start(f32[3,8,1,256]{3,2,1,0:T(1,128)S(1)} %get-tuple-element.137), channel_id=1, source_target_pairs={{32,0},{64,32},{96,64},{128,96},{160,128},{192,160},{224,192},{33,... | collective-permute-start | bytes 73736 | tf_op jit(solution)/shard_map/ppermute | solution.py:37
  303.2 4.9 %collective-permute-start.22 = (f32[3,8,1,256]{3,2,1,0:T(1,128)S(1)}, f32[3,8,1,256]{3,2,1,0:T(1,128)S(1)}, u32[]{:S(2)}, u32[]{:S(2)}) collective-permute-start(f32[3,8,1,256]{3,2,1,0:T(1,128)S(1)} %get-tuple-element.136), channel_id=1, source_target_pairs={{0,32},{32,64},{64,96},{96,128},{128,160},{160,192},{192,224},{1,3... | collective-permute-start | bytes 73736 | tf_op jit(solution)/shard_map/ppermute | solution.py:36
  308.3 8.7 %collective-permute-start.25 = (f32[3,8,18,1]{3,2,1,0:T(8,128)S(1)}, f32[3,8,18,1]{3,2,1,0:T(8,128)S(1)}, u32[]{:S(2)}, u32[]{:S(2)}) collective-permute-start(f32[3,8,18,1]{3,2,1,0:T(8,128)S(1)} %get-tuple-element.127), channel_id=1, source_target_pairs={{2,0},{4,2},{6,4},{8,6},{10,8},{12,10},{14,12},{16,14},{18,16},{20... | collective-permute-start | bytes 5192 | tf_op jit(solution)/shard_map/ppermute | solution.py:37
  312.6 5.6 %collective-permute-start.24 = (f32[3,8,18,1]{3,2,1,0:T(8,128)S(1)}, f32[3,8,18,1]{3,2,1,0:T(8,128)S(1)}, u32[]{:S(2)}, u32[]{:S(2)}) collective-permute-start(f32[3,8,18,1]{3,2,1,0:T(8,128)S(1)} %get-tuple-element.126), channel_id=1, source_target_pairs={{0,2},{2,4},{4,6},{6,8},{8,10},{10,12},{12,14},{14,16},{16,18},{18... | collective-permute-start | bytes 5192 | tf_op jit(solution)/shard_map/ppermute | solution.py:36
  318.3 7.1 %collective-permute-start.27 = (f32[3,1,18,258]{3,2,1,0:T(8,128)S(1)}, f32[3,1,18,258]{3,2,1,0:T(8,128)S(1)}, u32[]{:S(2)}, u32[]{:S(2)}) collective-permute-start(f32[3,1,18,258]{3,2,1,0:T(8,128)S(1)} %get-tuple-element.115), channel_id=1, source_target_pairs={{1,0},{3,2},{5,4},{7,6},{9,8},{11,10},{13,12},{15,14},{17,16},{19,... | collective-permute-start | bytes 167192 | tf_op jit(solution)/shard_map/ppermute | solution.py:37
  319.6 7.2 %collective-permute-start.26 = (f32[3,1,18,258]{3,2,1,0:T(8,128)S(1)}, f32[3,1,18,258]{3,2,1,0:T(8,128)S(1)}, u32[]{:S(2)}, u32[]{:S(2)}) collective-permute-start(f32[3,1,18,258]{3,2,1,0:T(8,128)S(1)} %get-tuple-element.114), channel_id=1, source_target_pairs={{0,1},{2,3},{4,5},{6,7},{8,9},{10,11},{12,13},{14,15},{16,17},{18,... | collective-permute-start | bytes 167192 | tf_op jit(solution)/shard_map/ppermute | solution.py:36
  (1 other events, 6.2 us)
